TPU v7x, 32 devices: a whole 2x2x4 slice. The times are simulated.
32 devices in a mesh: net: 4 (over y, x), line: 8 (over z, core).
Axes of the slice: x: 2, y: 2, z: 4, core: 2. Of those that a mesh axis runs over, the one named last changes fastest.
Arguments:
- conductance_inverse: float32 [4, 4096, 4096], P('net', 'line'), may hold values from -0.5 to 4.5, as said below
- prior_voltage: float32 [4, 96, 4096], P('net', None, 'line'), may hold values from -6 to 6
- sources: float32 [3, 4, 4096], P(None, 'net', 'line'), may hold values from -6 to 6
- fault_node: int32 [96], replicated, may hold values from 0 to 16383
- fault_conductance: float32 [96], replicated, may hold values from 0.5 to 4
- terminal_node: int32 [4, 3, 4096], P('net', None, 'line'), may hold values from 0 to 4095
- ownership: int32 [4, 4096], P('net', 'line'), may hold values from 0 to 1, as said below
- partner: int32 [4, 4096], P('net', 'line'), may hold values from 0 to 31, as said below
- delay_steps: int32 [4, 4096], P('net', 'line'), may hold values from 1 to 4, as said below
- surge_conductance: float32 [4, 4096], P('net', 'line'), may hold values from 0.2 to 1
- pole_wave: float32 [4, 6, 4096], P('net', None, 'line'), may hold values from 0.2 to 0.95
- residue_wave: float32 [4, 6, 3, 3, 4096], P('net', None, None, None, 'line'), may hold values from -1 to 1
- pole_admit: float32 [4, 6, 4096], P('net', None, 'line'), may hold values from 0.2 to 0.95
- residue_admit: float32 [4, 6, 3, 3, 4096], P('net', None, None, None, 'line'), may hold values from -1 to 1
- wave_state: float32 [4, 6, 3, 96, 4096], P('net', None, None, None, 'line'), may hold values from -4 to 4
- admit_state: float32 [4, 6, 3, 96, 4096], P('net', None, None, None, 'line'), may hold values from -4 to 4
- wave_history: float32 [4, 4, 3, 96, 4096], P('net', None, None, None, 'line'), may hold values from -6 to 6
Outputs:
- final_voltage: float32 [4, 96, 4096], P('net', None, 'line')
- end_current: float32 [4, 3, 96, 4096], P('net', None, None, 'line')
Inputs may be any that keep to these rules, and one draw needn't show every extreme that they name: `conductance_inverse`: each block is exactly symmetric. `ownership`: A slot is live exactly when the slot of the same number j % 512 at its partner owner is live; the number of live slots differs from owner to owner. The far end of slot j lies in the slot of the same number j % 512 at the partner owner, the partner of that slot is the first owner again, never the owner itself, and at most 17 live slots of one owner have the same partner; this many occur. `delay_steps`: equal at both ends of a line.
All inputs are finite; a program needn't handle non-finite values.
Results may differ from a plain program's by a relative error of at most 0.0003.
Values sent between devices are 32-bit elements; how exact they have to be, the bound alone decides.
A program may use at most 128 MiB of HBM per device.

v0:
```python
import jax
import jax.numpy as jnp
from jax import lax
from jax.sharding import PartitionSpec as P

STEPS = 3


def mix_residue(residue, vector):
    return (
        residue[:, :, 0, None, :] * vector[0]
        + residue[:, :, 1, None, :] * vector[1]
        + residue[:, :, 2, None, :] * vector[2]
    )


def select_delayed(buffer, delay_local):
    depth_count = buffer.shape[0]
    chosen = delay_local[None, :] == jnp.arange(1, depth_count + 1, dtype=jnp.int32)[:, None]
    return jnp.sum(jnp.where(chosen[:, None, None, :], buffer, 0.0), axis=0)


def terminal_values(voltage, terminal):
    picked = jnp.take(voltage, terminal.reshape(-1), axis=1)
    return jnp.moveaxis(picked.reshape(voltage.shape[0], 3, -1), 0, 1)


def spread_ends(history, terminal, node_count):
    values = jnp.moveaxis(history, 0, 1).reshape(history.shape[1], -1)
    return (
        jnp.zeros((history.shape[1], node_count), jnp.float32)
        .at[:, terminal.reshape(-1)]
        .add(values)
    )


def gather_full(block):
    return lax.all_gather(block, "line", axis=1, tiled=True)


def on_device(
    conductance_inverse,
    prior_voltage,
    sources,
    fault_node,
    fault_conductance,
    terminal_node,
    ownership,
    partner,
    delay_steps,
    surge_conductance,
    pole_wave,
    residue_wave,
    pole_admit,
    residue_admit,
    wave_state,
    admit_state,
    wave_history,
):
    inverse_block = conductance_inverse[0]
    row_count = inverse_block.shape[0]
    node_count = inverse_block.shape[1]
    line_index = lax.axis_index("line")
    net_index = lax.axis_index("net")
    offset = line_index * row_count
    net_count = lax.axis_size("net")
    line_count = lax.axis_size("line")
    devices = net_count * line_count
    slot_count = ownership.shape[1]
    capacity = (slot_count + devices - 2) // (devices - 1)
    is_live = ownership[0] > 0
    live_float = is_live.astype(jnp.float32)
    terminal = terminal_node[0]
    delay_local = delay_steps[0]
    surge_local = surge_conductance[0]
    partners = partner[0]
    slot_range = jnp.arange(slot_count, dtype=jnp.int32)
    earlier = (
        (partners[:, None] == partners[None, :])
        & is_live[None, :]
        & (slot_range[None, :] < slot_range[:, None])
    )
    slot_rank = jnp.sum(earlier.astype(jnp.int32), axis=1)
    position = jnp.where(is_live, partners * capacity + slot_rank, devices * capacity)
    scenario_range = jnp.arange(prior_voltage.shape[1], dtype=jnp.int32)
    fault_sub = fault_node // node_count
    fault_local = fault_node % node_count
    fault_here = (fault_sub == net_index) & (fault_local // row_count == line_index)
    wave_decay = pole_wave[0][:, None, None, :]
    admit_decay = pole_admit[0][:, None, None, :]
    wave_res = residue_wave[0]
    admit_res = residue_admit[0]
    voltage = gather_full(prior_voltage[0])
    voltage_rows = prior_voltage[0]
    wave_now = wave_state[0]
    admits = admit_state[0]
    history_buffer = wave_history[0]
    outgoing = None
    current = None
    for step_index in range(STEPS):
        terminal_prior = terminal_values(voltage, terminal)
        admits = admit_decay * admits + mix_residue(admit_res, terminal_prior)
        if step_index == 0:
            wave_now = wave_decay * wave_now + mix_residue(
                wave_res, select_delayed(history_buffer, delay_local)
            )
        else:
            shifted = jnp.concatenate(
                [jnp.zeros_like(history_buffer[:1]), history_buffer[:-1]], axis=0
            )
            wave_now = wave_decay * wave_now + mix_residue(
                wave_res, select_delayed(shifted, delay_local)
            )
            row_width = outgoing.shape[0] * outgoing.shape[1]
            packed = jnp.moveaxis(outgoing, 2, 0).reshape(slot_count, row_width)
            buffer = (
                jnp.zeros((devices * capacity, row_width), jnp.float32)
                .at[position]
                .set(packed, mode="drop")
            )
            arrived = lax.all_to_all(
                buffer, ("net", "line"), split_axis=0, concat_axis=0, tiled=True
            )
            picked_rows = arrived[jnp.minimum(position, devices * capacity - 1)]
            arrived = jnp.moveaxis(picked_rows.reshape(slot_count, 3, -1), 0, 2) * live_float
            newest = jnp.where((delay_local == 1)[None, None, :], arrived, 0.0)
            wave_now = wave_now + mix_residue(wave_res, newest)
            history_buffer = jnp.concatenate([arrived[None], shifted[1:]], axis=0)
        history = (jnp.sum(wave_now, axis=0) - jnp.sum(admits, axis=0)) * live_float
        injection = spread_ends(history, terminal, node_count)
        own_part = (
            lax.dynamic_slice_in_dim(injection, offset, row_count, 1)
            + sources[step_index, 0][None, :]
        )
        injection = lax.dynamic_update_slice_in_dim(injection, own_part, offset, 1)
        fault_value = voltage[scenario_range, fault_local]
        injection = injection.at[scenario_range, fault_local].add(
            jnp.where(fault_here, -fault_conductance * fault_value, 0.0)
        )
        summed = lax.psum(injection, "line")
        voltage_rows = lax.dot_general(
            summed,
            inverse_block,
            (((1,), (1,)), ((), ())),
            precision=lax.Precision.HIGHEST,
            preferred_element_type=jnp.float32,
        )
        voltage = gather_full(voltage_rows)
        terminal_now = terminal_values(voltage, terminal)
        if step_index + 1 < STEPS:
            outgoing = (2.0 * surge_local * terminal_now - history) * live_float
        else:
            current = (surge_local * terminal_now - history) * live_float
    return (voltage_rows[None], current[None])


def solution(mesh):
    return jax.shard_map(
        on_device,
        mesh=mesh,
        in_specs=(
            P("net", "line", None),
            P("net", None, "line"),
            P(None, "net", "line"),
            P(),
            P(),
            P("net", None, "line"),
            P("net", "line"),
            P("net", "line"),
            P("net", "line"),
            P("net", "line"),
            P("net", None, "line"),
            P("net", None, None, None, "line"),
            P("net", None, "line"),
            P("net", None, None, None, "line"),
            P("net", None, None, None, "line"),
            P("net", None, None, None, "line"),
            P("net", None, None, None, "line"),
        ),
        out_specs=(P("net", None, "line"), P("net", None, None, "line")),
        check_vma=False,
    )
```

profile of v0, /device:TPU:0, one launch (start us, length us, event | category | flops | bytes accessed | tf_op | source)
XLA Modules:
  0.0 577.8 jit_solution(13432879487147559588)
XLA Ops:
  32.9 8.7 %all-gather.12.cloned.1.call-done = f32[1,96,4096]{1,2,0:T(8,128)} async-done(((f32[1,96,512]{1,2,0:T(8,128)}), f32[1,96,4096]{1,2,0:T(8,128)}) %all-gather.12.cloned.1.call-update) | async-done | bytes 1572880 | tf_op jit(solution)/shard_map/all_gather | solution.py:38
  45.1 5.6 gather_fusion.5
  64.7 10.5 %scatter_custom_fusion = f32[96,4096]{0,1:T(8,128)} fusion(s32[1536]{0:T(1024)} %fusion.32, f32[1536,96]{1,0:T(8,128)} %copy.74, f32[]{:T(128)} %constant.37.clone.1), kind=kCustom, calls=%fused_computation.47 | custom fusion | flops 147456 | bytes 1573376 | tf_op jit(solution)/shard_map/scatter-add | solution.py:33
  81.1 12.2 %scatter_fusion = f32[96,4096]{1,0:T(8,128)} fusion(f32[96,4096]{1,0:T(8,128)} %copy.75, s32[96]{0:T(128)S(1)} %fusion.36, f32[96]{0:T(128)} %get-tuple-element.9), kind=kCustom, calls=%fused_computation.10 | custom fusion | flops 96 | bytes 1920 | tf_op jit(solution)/shard_map/scatter-add | solution.py:137
  93.6 61.2 %all-reduce.6.cloned.1.call-done = f32[96,4096]{1,0:T(8,128)} async-done(((f32[96,4096]{1,0:T(8,128)}), f32[96,4096]{1,0:T(8,128)}) %all-reduce.6.cloned.1.call-update) | async-done | bytes 1572880 | tf_op jit(solution)/shard_map/psum | solution.py:140
  154.8 12.7 %fusion.4 = f32[96,512]{1,0:T(8,128)} fusion(f32[96,4096]{1,0:T(8,128)} %all-reduce.6.cloned.1.call-done, f32[1,512,4096]{2,1,0:T(8,128)} %param.19), kind=kOutput, calls=%fused_computation.21 | convolution fusion | flops 2415919104 | bytes 10158080 | tf_op jit(solution)/shard_map/dot_general | solution.py:141
  174.4 17.7 %all-gather.6.cloned.1.call-done = f32[96,4096]{1,0:T(8,128)} async-done(((f32[96,512]{1,0:T(8,128)}), f32[96,4096]{1,0:T(8,128)}) %all-gather.6.cloned.1.call-update) | async-done | bytes 1572880 | tf_op jit(solution)/shard_map/all_gather | solution.py:38
  194.9 5.6 gather_fusion.6
  215.7 3.8 all-to-all-start
  234.3 4.2 fusion.11
  238.5 11.3 %all-to-all-done = f32[32,17,288]{2,1,0:T(8,128)} async-done(((f32[32,17,288]{2,1,0:T(8,128)}), f32[32,17,288]{2,1,0:T(8,128)}, u32[]{:S(2)}, u32[]{:S(2)}) %all-to-all-start) | async-done | bytes 626720 | tf_op jit(solution)/shard_map/all_to_all | solution.py:121
  256.8 3.9 fusion.38
  262.1 9.4 %scatter_custom_fusion.3 = f32[96,4096]{0,1:T(8,128)S(1)} fusion(s32[1536]{0:T(1024)} %fusion.32, f32[1536,96]{1,0:T(8,128)S(1)} %copy.84, f32[]{:T(128)} %constant.37.clone.1), kind=kCustom, calls=%fused_computation.45 | custom fusion | flops 147456 | bytes 1573376 | tf_op jit(solution)/shard_map/scatter-add | solution.py:33
  273.3 12.2 %scatter_fusion.1 = f32[96,4096]{1,0:T(8,128)} fusion(f32[96,4096]{1,0:T(8,128)} %copy.85, s32[96]{0:T(128)S(1)} %fusion.36, f32[96]{0:T(128)S(1)} %copy-done.45), kind=kCustom, calls=%fused_computation.13 | custom fusion | flops 96 | bytes 1920 | tf_op jit(solution)/shard_map/scatter-add | solution.py:137
  286.0 59.3 %all-reduce.8.cloned.1.call-done = f32[96,4096]{1,0:T(8,128)} async-done(((f32[96,4096]{1,0:T(8,128)}), f32[96,4096]{1,0:T(8,128)}) %all-reduce.8.cloned.1.call-update) | async-done | bytes 1572880 | tf_op jit(solution)/shard_map/psum | solution.py:140
  345.3 12.6 %fusion.2 = f32[96,512]{1,0:T(8,128)} fusion(f32[96,4096]{1,0:T(8,128)} %all-reduce.8.cloned.1.call-done, f32[1,512,4096]{2,1,0:T(8,128)} %param.19), kind=kOutput, calls=%fused_computation.19 | convolution fusion | flops 2415919104 | bytes 10158080 | tf_op jit(solution)/shard_map/dot_general | solution.py:141
  358.8 23.8 %all-gather.8.cloned.1.call-done = f32[96,4096]{1,0:T(8,128)} async-done(((f32[96,512]{1,0:T(8,128)}), f32[96,4096]{1,0:T(8,128)}) %all-gather.8.cloned.1.call-update) | async-done | bytes 1572880 | tf_op jit(solution)/shard_map/all_gather | solution.py:38
  412.3 4.8 add_reduce_fusion
  417.2 13.2 %all-to-all-done.1 = f32[32,17,288]{2,1,0:T(8,128)} async-done(((f32[32,17,288]{2,1,0:T(8,128)}), f32[32,17,288]{2,1,0:T(8,128)}, u32[]{:S(2)}, u32[]{:S(2)}) %all-to-all-start.1) | async-done | bytes 626720 | tf_op jit(solution)/shard_map/all_to_all | solution.py:121
  442.0 9.4 %scatter_custom_fusion.6 = f32[96,4096]{0,1:T(8,128)S(1)} fusion(s32[1536]{0:T(1024)} %fusion.32, f32[1536,96]{1,0:T(8,128)S(1)} %copy.94, f32[]{:T(128)} %constant.37.clone.1), kind=kCustom, calls=%fused_computation.43 | custom fusion | flops 147456 | bytes 1573376 | tf_op jit(solution)/shard_map/scatter-add | solution.py:33
  453.2 12.2 %scatter_fusion.2 = f32[96,4096]{1,0:T(8,128)} fusion(f32[96,4096]{1,0:T(8,128)} %copy.95, s32[96]{0:T(128)S(1)} %fusion.36, f32[96]{0:T(128)S(1)} %copy-done.44), kind=kCustom, calls=%fused_computation.16 | custom fusion | flops 96 | bytes 1920 | tf_op jit(solution)/shard_map/scatter-add | solution.py:137
  465.7 59.5 %all-reduce.10.cloned.1.call-done = f32[96,4096]{1,0:T(8,128)} async-done(((f32[96,4096]{1,0:T(8,128)}), f32[96,4096]{1,0:T(8,128)}) %all-reduce.10.cloned.1.call-update) | async-done | bytes 1572880 | tf_op jit(solution)/shard_map/psum | solution.py:140
  525.2 12.7 %fusion = f32[96,512]{1,0:T(8,128)} fusion(f32[96,4096]{1,0:T(8,128)} %all-reduce.10.cloned.1.call-done, f32[1,512,4096]{2,1,0:T(8,128)} %param.19), kind=kOutput, calls=%fused_computation.17 | convolution fusion | flops 2415919104 | bytes 10158080 | tf_op jit(solution)/shard_map/dot_general | solution.py:141
  537.9 24.6 %all-gather.10.cloned.1.call-done = f32[96,4096]{1,0:T(8,128)} async-done(((f32[96,512]{1,0:T(8,128)}), f32[96,4096]{1,0:T(8,128)}) %all-gather.10.cloned.1.call-update) | async-done | bytes 1572880 | tf_op jit(solution)/shard_map/all_gather | solution.py:38
  (215 shorter events, 151.6 us)
Async XLA Ops:
  7.2 18.5 %copy-start.46 = (s32[96]{0:T(128)S(1)}, s32[96]{0:T(128)}, u32[]{:S(2)}) copy-start(s32[96]{0:T(128)} %param.22) | copy-start | bytes 1156
  7.2 23.8 %copy-start.2 = (f32[1,6,3,96,512]{4,3,2,1,0:T(8,128)S(1)}, f32[1,6,3,96,512]{4,3,2,1,0:T(8,128)}, u32[]{:S(2)}) copy-start(f32[1,6,3,96,512]{4,3,2,1,0:T(8,128)} %param.33) | copy-start | bytes 10616836
  7.2 34.3 %all-gather.12.cloned.1.call-start = ((), (), s32[]{:S(2)}) async-start(), calls=%async_computation.8 | async-start | bytes 2359296 | tf_op jit(solution)/shard_map/all_gather | solution.py:38
  9.2 145.6 %all-reduce.6.cloned.1.call-start = ((), (), s32[]{:S(2)}) async-start(), calls=%async_computation.2 | async-start | bytes 3145728 | tf_op jit(solution)/shard_map/psum | solution.py:140
  12.5 11.2 %copy-start.35 = (s32[1536]{0:T(1024)}, s32[1536]{0:T(1024)S(1)}, u32[]{:S(2)}) copy-start(s32[1536]{0:T(1024)S(1)} %reshape_squeeze.5) | copy-start | bytes 18436
  20.2 10.8 %copy-start.25 = (f32[6,3,1,512]{3,1,2,0:T(4,128)S(1)}, f32[6,3,1,512]{3,1,2,0:T(4,128)}, u32[]{:S(2)}) copy-start(f32[6,3,1,512]{3,1,2,0:T(4,128)} %copy.124) | copy-start | bytes 110596
  20.2 10.8 %copy-start.31 = (f32[1,6,512]{2,1,0:T(8,128)S(1)}, f32[1,6,512]{2,1,0:T(8,128)}, u32[]{:S(2)}) copy-start(f32[1,6,512]{2,1,0:T(8,128)} %copy.126) | copy-start | bytes 36868
  50.7 7.7 %copy-start = (f32[1,6,3,96,512]{4,3,2,1,0:T(8,128)S(1)}, f32[1,6,3,96,512]{4,3,2,1,0:T(8,128)}, u32[]{:S(2)}) copy-start(f32[1,6,3,96,512]{4,3,2,1,0:T(8,128)} %param.34) | copy-start | bytes 10616836
  93.4 98.7 %all-gather.6.cloned.1.call-start = ((), (), s32[]{:S(2)}) async-start(), calls=%async_computation.3 | async-start | bytes 1769472 | tf_op jit(solution)/shard_map/all_gather | solution.py:38
  215.7 34.1 %all-to-all-start = ((f32[32,17,288]{2,1,0:T(8,128)}), f32[32,17,288]{2,1,0:T(8,128)}, u32[]{:S(2)}, u32[]{:S(2)}) async-start(f32[32,17,288]{2,1,0:T(8,128)} %all_to_all.16), calls=%async_computation | async-start | bytes 2359296 | tf_op jit(solution)/shard_map/all_to_all | solution.py:121
  219.5 125.8 %all-reduce.8.cloned.1.call-start = ((), (), s32[]{:S(2)}) async-start(), calls=%async_computation.4 | async-start | bytes 3145728 | tf_op jit(solution)/shard_map/psum | solution.py:140
  260.8 10.7 %copy-start.41 = (f32[1,1,512]{2,1,0:T(1,128)S(1)}, f32[1,1,512]{2,1,0:T(1,128)}, u32[]{:S(2)}) copy-start(f32[1,1,512]{2,1,0:T(1,128)} %get-tuple-element.45) | copy-start | bytes 6148
  261.8 11.6 %copy-start.45 = (f32[96]{0:T(128)S(1)}, f32[96]{0:T(128)}, u32[]{:S(2)}) copy-start(f32[96]{0:T(128)} %multiply_select_fusion.1) | copy-start | bytes 1156
  285.6 72.4 %copy-start.18 = (f32[3,96,512]{2,1,0:T(8,128)S(1)}, f32[3,96,512]{2,1,0:T(8,128)}, u32[]{:S(2)}) copy-start(f32[3,96,512]{2,1,0:T(8,128)} %get-tuple-element.3) | copy-start | bytes 1769476
  285.6 97.0 %all-gather.8.cloned.1.call-start = ((), (), s32[]{:S(2)}) async-start(), calls=%async_computation.5 | async-start | bytes 1769472 | tf_op jit(solution)/shard_map/all_gather | solution.py:38
  358.0 26.5 %copy-start.33 = (s32[2048]{0:T(1024)S(1)}, s32[2048]{0:T(1024)}, u32[]{:S(2)}) copy-start(s32[2048]{0:T(1024)} %pad_clamp_fusion) | copy-start | bytes 24580
  384.4 5.4 copy-start.11
  393.8 18.5 %copy-start.1 = (f32[1,6,3,96,512]{4,3,2,1,0:T(8,128)S(1)}, f32[1,6,3,96,512]{4,3,2,1,0:T(8,128)}, u32[]{:S(2)}) copy-start(f32[1,6,3,96,512]{4,3,2,1,0:T(8,128)} %param.34) | copy-start | bytes 10616836
  396.3 34.1 %all-to-all-start.1 = ((f32[32,17,288]{2,1,0:T(8,128)}), f32[32,17,288]{2,1,0:T(8,128)}, u32[]{:S(2)}, u32[]{:S(2)}) async-start(f32[32,17,288]{2,1,0:T(8,128)} %all_to_all.19), calls=%async_computation.1 | async-start | bytes 2359296 | tf_op jit(solution)/shard_map/all_to_all | solution.py:121
  400.1 125.1 %all-reduce.10.cloned.1.call-start = ((), (), s32[]{:S(2)}) async-start(), calls=%async_computation.6 | async-start | bytes 3145728 | tf_op jit(solution)/shard_map/psum | solution.py:140
  440.8 10.5 %copy-start.40 = (f32[1,1,512]{2,1,0:T(1,128)S(1)}, f32[1,1,512]{2,1,0:T(1,128)}, u32[]{:S(2)}) copy-start(f32[1,1,512]{2,1,0:T(1,128)} %get-tuple-element.43) | copy-start | bytes 6148
  441.7 11.5 %copy-start.44 = (f32[96]{0:T(128)S(1)}, f32[96]{0:T(128)}, u32[]{:S(2)}) copy-start(f32[96]{0:T(128)} %multiply_select_fusion) | copy-start | bytes 1156
  465.5 97.0 %all-gather.10.cloned.1.call-start = ((), (), s32[]{:S(2)}) async-start(), calls=%async_computation.7 | async-start | bytes 1769472 | tf_op jit(solution)/shard_map/all_gather | solution.py:38
  537.9 26.5 %copy-start.34 = (s32[2048]{0:T(1024)S(1)}, s32[2048]{0:T(1024)}, u32[]{:S(2)}) copy-start(s32[2048]{0:T(1024)} %pad_clamp_fusion) | copy-start | bytes 24580
  (33 other events, 88.0 us)
Sparse Core Ops, SparseCore 0:
  9.6 31.8 all-gather.11
  93.5 61.2 all-reduce.5
  167.6 24.4 all-gather.5
  285.7 59.5 all-reduce.7
  358.1 24.4 all-gather.7
  465.6 59.5 all-reduce.9
  538.0 24.4 all-gather.9
where the time goes:
time: 587 us; the launch traced here: 578 us
  waiting for transfers between devices  279 us (48%)
  other arithmetic  122 us (21%)
  local copies, waits for them, and re-layouts  115 us (20%)
  matrix products  38 us (6%)
  between operations  15.2 us (3%)
  starting transfers between devices  9.15 us (2%)
    psum x3, waiting for transfers between devices, on_device(): summed = lax.psum(injection, 'line')  180 us
    all_gather x4, waiting for transfers between devices, gather_full(): return lax.all_gather(block, 'line', axis=1, tiled=True)  74.8 us
    dot_general x3, matrix products, on_device(): lax.dot_general(summed, inverse_block, (((1,), (1,)), ((), ())), precisio...  38 us
    scatter-add x3, other arithmetic, on_device(): injection.at[scenario_range, fault_local]  36.6 us
    scatter-add x3, other arithmetic, spread_ends(): return jnp.zeros((history.shape[1], node_count), jnp.float32).at[:, termi...  29.3 us
    all_to_all x2, waiting for transfers between devices, on_device(): lax.all_to_all(buffer, ('net', 'line'), split_axis=0, concat_axis=0, tile...  24.6 us
    reduce_sum x6, other arithmetic, on_device(): history = (jnp.sum(wave_now, axis=0) - jnp.sum(admits, axis=0)) * live_float  20.3 us
    gather x4, local copies, waits for them, and re-layouts, terminal_values(): picked = jnp.take(voltage, terminal.reshape(-1), axis=1)  18.5 us
  transfers between devices with their start and end apart: 9, of which 9 were waited for; matrix products, arithmetic and copies ran while one was open for 11% of the time, Pallas kernels for 0%

commit v1 on v0

--- a/solution.py
+++ b/solution.py
@@ -2,6 +2,7 @@
 import jax.numpy as jnp
 from jax import lax
 from jax.sharding import PartitionSpec as P
+from jax.lax import all_to_all, axis_size
 
 STEPS = 3
 
@@ -35,7 +36,9 @@
 
 
 def gather_full(block):
-    return lax.all_gather(block, "line", axis=1, tiled=True)
+    return jnp.concatenate(
+        all_to_all(jnp.stack([block for _ in range(axis_size("line"))]), "line", 0, 0), axis=1
+    )
 
 
 def on_device(

time: 587 us -> 646 us (1.10)
  blocking collectives: 0 us -> 40.9 us
  starting transfers between devices: 9.15 us -> 22 us
  waiting for transfers between devices: 279 us -> 291 us
    all_to_all x0 -> x3, waiting for transfers between devices: none -> 82.1 us  [gather_full(): all_to_all(jnp.stack([block for _ in range(axis_size('line'))]), 'line',...]
    all_gather x4 -> x0, waiting for transfers between devices: 74.8 us -> none  [gather_full(): return lax.all_gather(block, 'line', axis=1, tiled=True)]
    all_to_all x0 -> x1, blocking collectives: none -> 40.9 us  [gather_full(): all_to_all(jnp.stack([block for _ in range(axis_size('line'))]), 'line',...]
    all_to_all x0 -> x3, starting transfers between devices: none -> 14.3 us  [gather_full(): all_to_all(jnp.stack([block for _ in range(axis_size('line'))]), 'line',...]
    reshape x0 -> x4, local copies, waits for them, and re-layouts: none -> 8.29 us  [gather_full(): jnp.concatenate(all_to_all(jnp.stack([block for _ in range(axis_size('lin...]
    unnamed x105 -> x108, local copies, waits for them, and re-layouts: 14.6 us -> 13.2 us
  transfers between devices with their start and end apart: 9 -> 8, of which waited for: 9 -> 8; matrix products, arithmetic and copies ran while one was open for 11% -> 10% of each run, Pallas kernels for 0% -> 0%
where the time goes in v1:
time: 646 us; the launch traced here: 637 us
  waiting for transfers between devices  291 us (45%)
  other arithmetic  120 us (19%)
  local copies, waits for them, and re-layouts  117 us (18%)
  blocking collectives  40.9 us (6%)
  matrix products  32.2 us (5%)
  starting transfers between devices  22 us (3%)
  between operations  15 us (2%)
    psum x3, waiting for transfers between devices, on_device(): summed = lax.psum(injection, 'line')  180 us
    all_to_all x3, waiting for transfers between devices, gather_full(): all_to_all(jnp.stack([block for _ in range(axis_size('line'))]), 'line',...  82.1 us
    all_to_all x1, blocking collectives, gather_full(): all_to_all(jnp.stack([block for _ in range(axis_size('line'))]), 'line',...  40.9 us
    scatter-add x3, other arithmetic, on_device(): injection.at[scenario_range, fault_local]  36.6 us
    dot_general x3, matrix products, on_device(): lax.dot_general(summed, inverse_block, (((1,), (1,)), ((), ())), precisio...  32.2 us
    scatter-add x3, other arithmetic, spread_ends(): return jnp.zeros((history.shape[1], node_count), jnp.float32).at[:, termi...  30.2 us
    all_to_all x2, waiting for transfers between devices, on_device(): lax.all_to_all(buffer, ('net', 'line'), split_axis=0, concat_axis=0, tile...  28 us
    reduce_sum x6, other arithmetic, on_device(): history = (jnp.sum(wave_now, axis=0) - jnp.sum(admits, axis=0)) * live_float  20.3 us
  transfers between devices with their start and end apart: 8, of which 8 were waited for; matrix products, arithmetic and copies ran while one was open for 10% of the time, Pallas kernels for 0%

profile of v1, /device:TPU:0, one launch (start us, length us, event | category | flops | bytes accessed | tf_op | source)
XLA Modules:
  0.0 637.2 jit_solution(6135681208076646044)
XLA Ops:
  9.5 6.4 all-to-all-start
  38.2 15.5 %all-to-all-done = f32[8,96,512]{2,1,0:T(8,128)} async-done(((f32[8,96,512]{2,1,0:T(8,128)}), f32[8,96,512]{2,1,0:T(8,128)}, u32[]{:S(2)}, u32[]{:S(2)}) %all-to-all-start) | async-done | bytes 1572896 | tf_op jit(solution)/shard_map/all_to_all | solution.py:40
  75.1 11.0 %scatter_custom_fusion = f32[96,4096]{0,1:T(8,128)} fusion(s32[1536]{0:T(1024)} %fusion.32, f32[1536,96]{1,0:T(8,128)} %copy.103, f32[]{:T(128)} %constant.37.clone.1), kind=kCustom, calls=%fused_computation.47 | custom fusion | flops 147456 | bytes 1573376 | tf_op jit(solution)/shard_map/scatter-add | solution.py:34
  91.9 12.2 %scatter_fusion = f32[96,4096]{1,0:T(8,128)} fusion(f32[96,4096]{1,0:T(8,128)} %copy.104, s32[96]{0:T(128)S(1)} %fusion.36, f32[96]{0:T(128)} %get-tuple-element.9), kind=kCustom, calls=%fused_computation.10 | custom fusion | flops 96 | bytes 1920 | tf_op jit(solution)/shard_map/scatter-add | solution.py:140
  104.2 61.0 %all-reduce.6.cloned.1.call-done = f32[96,4096]{1,0:T(8,128)} async-done(((f32[96,4096]{1,0:T(8,128)}), f32[96,4096]{1,0:T(8,128)}) %all-reduce.6.cloned.1.call-update) | async-done | bytes 1572880 | tf_op jit(solution)/shard_map/psum | solution.py:143
  165.2 10.7 %fusion.4 = f32[96,512]{1,0:T(8,128)S(1)} fusion(f32[96,4096]{1,0:T(8,128)} %all-reduce.6.cloned.1.call-done, f32[1,512,4096]{2,1,0:T(8,128)} %param.19), kind=kOutput, calls=%fused_computation.21 | convolution fusion | flops 2415919104 | bytes 10158080 | tf_op jit(solution)/shard_map/dot_general | solution.py:144
  177.3 4.3 all-to-all-start.1
  188.5 30.8 %all-to-all-done.1 = f32[8,96,512]{2,1,0:T(8,128)} async-done(((f32[8,96,512]{2,1,0:T(8,128)}), f32[8,96,512]{2,1,0:T(8,128)}, u32[]{:S(2)}, u32[]{:S(2)}) %all-to-all-start.1) | async-done | bytes 1572896 | tf_op jit(solution)/shard_map/all_to_all | solution.py:40
  222.2 5.6 gather_fusion.6
  261.2 4.2 fusion.11
  265.4 11.3 %all-to-all-done.2 = f32[32,17,288]{2,1,0:T(8,128)} async-done(((f32[32,17,288]{2,1,0:T(8,128)}), f32[32,17,288]{2,1,0:T(8,128)}, u32[]{:S(2)}, u32[]{:S(2)}) %all-to-all-start.2) | async-done | bytes 626720 | tf_op jit(solution)/shard_map/all_to_all | solution.py:124
  282.7 3.9 fusion.38
  288.0 9.8 %scatter_custom_fusion.3 = f32[96,4096]{0,1:T(8,128)S(1)} fusion(s32[1536]{0:T(1024)} %fusion.32, f32[1536,96]{1,0:T(8,128)} %copy.113, f32[]{:T(128)} %constant.37.clone.1), kind=kCustom, calls=%fused_computation.45 | custom fusion | flops 147456 | bytes 1573376 | tf_op jit(solution)/shard_map/scatter-add | solution.py:34
  299.7 12.2 %scatter_fusion.1 = f32[96,4096]{1,0:T(8,128)} fusion(f32[96,4096]{1,0:T(8,128)} %copy.114, s32[96]{0:T(128)S(1)} %fusion.36, f32[96]{0:T(128)S(1)} %copy-done.48), kind=kCustom, calls=%fused_computation.13 | custom fusion | flops 96 | bytes 1920 | tf_op jit(solution)/shard_map/scatter-add | solution.py:140
  311.9 59.7 %all-reduce.8.cloned.1.call-done = f32[96,4096]{1,0:T(8,128)} async-done(((f32[96,4096]{1,0:T(8,128)}), f32[96,4096]{1,0:T(8,128)}) %all-reduce.8.cloned.1.call-update) | async-done | bytes 1572880 | tf_op jit(solution)/shard_map/psum | solution.py:143
  371.6 10.7 %fusion.2 = f32[96,512]{1,0:T(8,128)S(1)} fusion(f32[96,4096]{1,0:T(8,128)} %all-reduce.8.cloned.1.call-done, f32[1,512,4096]{2,1,0:T(8,128)} %param.19), kind=kOutput, calls=%fused_computation.19 | convolution fusion | flops 2415919104 | bytes 10158080 | tf_op jit(solution)/shard_map/dot_general | solution.py:144
  389.4 35.8 %all-to-all-done.3 = f32[8,96,512]{2,1,0:T(8,128)S(1)} async-done(((f32[8,96,512]{2,1,0:T(8,128)}), f32[8,96,512]{2,1,0:T(8,128)S(1)}, u32[]{:S(2)}, u32[]{:S(2)}) %all-to-all-start.3) | async-done | bytes 1572896 | tf_op jit(solution)/shard_map/all_to_all | solution.py:40
  453.9 4.8 add_reduce_fusion
  458.7 16.7 %all-to-all-done.4 = f32[32,17,288]{2,1,0:T(8,128)} async-done(((f32[32,17,288]{2,1,0:T(8,128)}), f32[32,17,288]{2,1,0:T(8,128)}, u32[]{:S(2)}, u32[]{:S(2)}) %all-to-all-start.4) | async-done | bytes 626720 | tf_op jit(solution)/shard_map/all_to_all | solution.py:124
  486.9 9.4 %scatter_custom_fusion.6 = f32[96,4096]{0,1:T(8,128)S(1)} fusion(s32[1536]{0:T(1024)} %fusion.32, f32[1536,96]{1,0:T(8,128)S(1)} %copy.123, f32[]{:T(128)} %constant.37.clone.1), kind=kCustom, calls=%fused_computation.43 | custom fusion | flops 147456 | bytes 1573376 | tf_op jit(solution)/shard_map/scatter-add | solution.py:34
  498.1 12.2 %scatter_fusion.2 = f32[96,4096]{1,0:T(8,128)} fusion(f32[96,4096]{1,0:T(8,128)} %copy.124, s32[96]{0:T(128)S(1)} %fusion.36, f32[96]{0:T(128)S(1)} %copy-done.47), kind=kCustom, calls=%fused_computation.16 | custom fusion | flops 96 | bytes 1920 | tf_op jit(solution)/shard_map/scatter-add | solution.py:140
  510.3 59.7 %all-reduce.10.cloned.1.call-done = f32[96,4096]{1,0:T(8,128)} async-done(((f32[96,4096]{1,0:T(8,128)}), f32[96,4096]{1,0:T(8,128)}) %all-reduce.10.cloned.1.call-update) | async-done | bytes 1572880 | tf_op jit(solution)/shard_map/psum | solution.py:143
  570.1 10.7 %fusion = f32[96,512]{1,0:T(8,128)S(1)} fusion(f32[96,4096]{1,0:T(8,128)} %all-reduce.10.cloned.1.call-done, f32[1,512,4096]{2,1,0:T(8,128)} %param.19), kind=kOutput, calls=%fused_computation.17 | convolution fusion | flops 2415919104 | bytes 10158080 | tf_op jit(solution)/shard_map/dot_general | solution.py:144
  581.0 40.9 %all_to_all.44 = f32[8,96,512]{2,1,0:T(8,128)} all-to-all(f32[8,96,512]{2,1,0:T(8,128)S(1)} %stack.11), channel_id=1, replica_groups=mesh['net'=4,'line'=8] {'line'}, dimensions={0} | all-to-all | bytes 3145728 | tf_op jit(solution)/shard_map/all_to_all | solution.py:40
  (218 shorter events, 162.5 us)
Async XLA Ops:
  7.2 21.1 %copy-start.43 = (s32[1,512]{1,0:T(1,128)S(1)}, s32[1,512]{1,0:T(1,128)}, u32[]{:S(2)}) copy-start(s32[1,512]{1,0:T(1,128)} %param.27) | copy-start | bytes 6148
  9.5 44.3 %all-to-all-start = ((f32[8,96,512]{2,1,0:T(8,128)}), f32[8,96,512]{2,1,0:T(8,128)}, u32[]{:S(2)}, u32[]{:S(2)}) async-start(f32[8,96,512]{2,1,0:T(8,128)} %stack.8), calls=%async_computation | async-start | bytes 3145728 | tf_op jit(solution)/shard_map/all_to_all | solution.py:40
  15.8 20.5 %copy-start.2 = (f32[1,6,3,96,512]{4,3,2,1,0:T(8,128)S(1)}, f32[1,6,3,96,512]{4,3,2,1,0:T(8,128)}, u32[]{:S(2)}) copy-start(f32[1,6,3,96,512]{4,3,2,1,0:T(8,128)} %param.33) | copy-start | bytes 10616836
  15.8 149.3 %all-reduce.6.cloned.1.call-start = ((), (), s32[]{:S(2)}) async-start(), calls=%async_computation.6 | async-start | bytes 3145728 | tf_op jit(solution)/shard_map/psum | solution.py:143
  17.8 10.5 %copy-start.33 = (s32[1536]{0:T(1024)}, s32[1536]{0:T(1024)S(1)}, u32[]{:S(2)}) copy-start(s32[1536]{0:T(1024)S(1)} %reshape_squeeze.5) | copy-start | bytes 18436
  25.6 10.7 %copy-start.21 = (f32[6,3,1,512]{3,1,2,0:T(4,128)S(1)}, f32[6,3,1,512]{3,1,2,0:T(4,128)}, u32[]{:S(2)}) copy-start(f32[6,3,1,512]{3,1,2,0:T(4,128)} %copy.153) | copy-start | bytes 110596
  25.6 10.7 %copy-start.28 = (f32[1,6,512]{2,1,0:T(8,128)S(1)}, f32[1,6,512]{2,1,0:T(8,128)}, u32[]{:S(2)}) copy-start(f32[1,6,512]{2,1,0:T(8,128)} %copy.155) | copy-start | bytes 36868
  38.2 19.2 %copy-start.30 = (s32[2048]{0:T(1024)S(1)}, s32[2048]{0:T(1024)}, u32[]{:S(2)}) copy-start(s32[2048]{0:T(1024)} %pad_clamp_fusion) | copy-start | bytes 24580
  177.3 42.1 %all-to-all-start.1 = ((f32[8,96,512]{2,1,0:T(8,128)}), f32[8,96,512]{2,1,0:T(8,128)}, u32[]{:S(2)}, u32[]{:S(2)}) async-start(f32[8,96,512]{2,1,0:T(8,128)} %stack.9), calls=%async_computation.1 | async-start | bytes 3145728 | tf_op jit(solution)/shard_map/all_to_all | solution.py:40
  242.9 33.8 %all-to-all-start.2 = ((f32[32,17,288]{2,1,0:T(8,128)}), f32[32,17,288]{2,1,0:T(8,128)}, u32[]{:S(2)}, u32[]{:S(2)}) async-start(f32[32,17,288]{2,1,0:T(8,128)} %all_to_all.30), calls=%async_computation.2 | async-start | bytes 2359296 | tf_op jit(solution)/shard_map/all_to_all | solution.py:124
  246.5 125.1 %all-reduce.8.cloned.1.call-start = ((), (), s32[]{:S(2)}) async-start(), calls=%async_computation.7 | async-start | bytes 3145728 | tf_op jit(solution)/shard_map/psum | solution.py:143
  286.6 11.2 %copy-start.41 = (f32[1,1,512]{2,1,0:T(1,128)S(1)}, f32[1,1,512]{2,1,0:T(1,128)}, u32[]{:S(2)}) copy-start(f32[1,1,512]{2,1,0:T(1,128)} %get-tuple-element.45) | copy-start | bytes 6148
  286.8 12.9 %copy-start.48 = (f32[96]{0:T(128)S(1)}, f32[96]{0:T(128)}, u32[]{:S(2)}) copy-start(f32[96]{0:T(128)} %multiply_select_fusion.1) | copy-start | bytes 1156
  383.7 46.2 %copy-start.31 = (s32[2048]{0:T(1024)S(1)}, s32[2048]{0:T(1024)}, u32[]{:S(2)}) copy-start(s32[2048]{0:T(1024)} %pad_clamp_fusion) | copy-start | bytes 24580
  383.7 41.4 %all-to-all-start.3 = ((f32[8,96,512]{2,1,0:T(8,128)}), f32[8,96,512]{2,1,0:T(8,128)S(1)}, u32[]{:S(2)}, u32[]{:S(2)}) async-start(f32[8,96,512]{2,1,0:T(8,128)} %stack.10), calls=%async_computation.3 | async-start | bytes 3145728 | tf_op jit(solution)/shard_map/all_to_all | solution.py:40
  439.2 13.6 %copy-start.46 = (f32[96]{0:T(128)S(1)}, f32[96]{0:T(128)}, u32[]{:S(2)}) copy-start(f32[96]{0:T(128)} %param.23) | copy-start | bytes 1156
  439.2 14.7 %copy-start.1 = (f32[1,6,3,96,512]{4,3,2,1,0:T(8,128)S(1)}, f32[1,6,3,96,512]{4,3,2,1,0:T(8,128)}, u32[]{:S(2)}) copy-start(f32[1,6,3,96,512]{4,3,2,1,0:T(8,128)} %param.34) | copy-start | bytes 10616836
  441.6 33.8 %all-to-all-start.4 = ((f32[32,17,288]{2,1,0:T(8,128)}), f32[32,17,288]{2,1,0:T(8,128)}, u32[]{:S(2)}, u32[]{:S(2)}) async-start(f32[32,17,288]{2,1,0:T(8,128)} %all_to_all.34), calls=%async_computation.4 | async-start | bytes 2359296 | tf_op jit(solution)/shard_map/all_to_all | solution.py:124
  445.2 124.9 %all-reduce.10.cloned.1.call-start = ((), (), s32[]{:S(2)}) async-start(), calls=%async_computation.8 | async-start | bytes 3145728 | tf_op jit(solution)/shard_map/psum | solution.py:143
  453.9 22.9 %copy-start.38 = (s32[1024]{0:T(1024)S(1)}, s32[1024]{0:T(1024)}, u32[]{:S(2)}) copy-start(s32[1024]{0:T(1024)} %pad_clamp_fusion.1) | copy-start | bytes 12292
  485.8 10.5 %copy-start.40 = (f32[1,1,512]{2,1,0:T(1,128)S(1)}, f32[1,1,512]{2,1,0:T(1,128)}, u32[]{:S(2)}) copy-start(f32[1,1,512]{2,1,0:T(1,128)} %get-tuple-element.43) | copy-start | bytes 6148
  486.6 11.5 %copy-start.47 = (f32[96]{0:T(128)S(1)}, f32[96]{0:T(128)}, u32[]{:S(2)}) copy-start(f32[96]{0:T(128)} %multiply_select_fusion) | copy-start | bytes 1156
  580.8 43.0 %copy-start.27 = (f32[96,512]{1,0:T(8,128)}, f32[96,512]{1,0:T(8,128)S(1)}, u32[]{:S(2)}) copy-start(f32[96,512]{1,0:T(8,128)S(1)} %fusion) | copy-start | bytes 589828
  581.0 42.8 %copy-start.32 = (s32[2048]{0:T(1024)S(1)}, s32[2048]{0:T(1024)}, u32[]{:S(2)}) copy-start(s32[2048]{0:T(1024)} %pad_clamp_fusion) | copy-start | bytes 24580
  (34 other events, 100.7 us)
Sparse Core Ops, SparseCore 0:
  104.3 60.8 all-reduce.5
  312.0 59.5 all-reduce.7
  510.5 59.5 all-reduce.9
